TPU v7x, 256 devices: a whole 4x4x8 slice. The times are simulated.
256 devices in a mesh: coil: 4 (over z_lo), spoke: 64 (over y, z_hi, x, core).
Axes of the slice: x: 4, y: 4, z: 8 (z_hi: 2, z_lo: 4; z = z_hi * 4 + z_lo), core: 2. Of those that a mesh axis runs over, the one named last changes fastest.
Arguments:
- image: float32 [256, 2, 2, 256], P('spoke'), may hold values from -6 to 6
- residual: float32 [256, 2, 2, 256], P('spoke'), may hold values from -12 to 12
- direction: float32 [256, 2, 2, 256], P('spoke'), may hold values from -12 to 12
- coil_maps: bfloat16 [256, 32, 2, 2, 256], P(None, 'coil'), may hold values from -0.75 to 0.75
- interp_weights: bfloat16 [512, 128, 2048], P('spoke'), may hold values from -0.125 to 0.125
- tile_index: int32 [512], P('spoke'), may hold values from 0 to 31
Outputs:
- new_image: float32 [256, 2, 2, 256], P('spoke')
- new_residual: float32 [256, 2, 2, 256], P('spoke')
- new_direction: float32 [256, 2, 2, 256], P('spoke')
All inputs are finite; a program needn't handle non-finite values.
Results may differ from a plain program's by a relative error of at most 0.0017.
Values may be sent and summed in bfloat16 or wider, within the bound.
A program may use at most 128 MiB of HBM per device.

v0:
```python
import math

import jax
import jax.numpy as jnp
import numpy as np
from jax import lax
from jax.experimental import pallas as pl
from jax.experimental.pallas import tpu as pltpu
from jax.sharding import PartitionSpec as P

F32, BF16 = jnp.float32, jnp.bfloat16
MESH = pl.DeviceIdType.MESH
ridge = 0.1


class Place:
    def __init__(self):
        self.coil = lax.axis_index("coil")
        self.spoke = lax.axis_index("spoke")
        self.core = self.spoke % 2
        self.x = (self.spoke // 2) % 4
        self.hi = (self.spoke // 8) % 2
        self.y = self.spoke // 16
        self.z = self.hi * 4 + self.coil
        self.sibling = self.spoke + 1 - 2 * self.core
        self.other = self.spoke + 8 - 16 * self.hi

    def chip(self, j):
        q = (self.y * 4 + self.x + j) % 16
        return (q // 4) * 16 + self.hi * 8 + (q % 4) * 2 + self.core

    def in_plane(self, j):
        return (self.y * 8 + self.x * 2 + self.core + j) % 32


def spoke_of(q, hi):
    return (q // 8) * 16 + hi * 8 + q % 8


def signal(device):
    pl.semaphore_signal(pltpu.get_barrier_semaphore(), inc=1, device_id=device, device_id_type=MESH)


def remote(src, dst, send_sem, recv_sem, device):
    return pltpu.make_async_remote_copy(
        src_ref=src, dst_ref=dst, send_sem=send_sem, recv_sem=recv_sem,
        device_id=device, device_id_type=MESH,
    )


def wave_block():
    n = 256
    q = (np.arange(n)[:, None] * np.arange(n)[None, :]) % n
    ang = q.astype(np.float32) * np.float32(2.0 * math.pi / n)
    c = (np.cos(ang) * np.float32(1.0 / math.sqrt(n))).astype(jnp.bfloat16)
    s = (np.sin(ang) * np.float32(1.0 / math.sqrt(n))).astype(jnp.bfloat16)
    return np.concatenate([np.concatenate([c, s], 1), np.concatenate([-s, c], 1)], 0)

def dot(a, b, dims=(((1,), (0,)), ((), ()))):
    return lax.dot_general(a, b, dims, preferred_element_type=F32)

def tables(tile_ref, wave, tf, tft):
    row = lax.broadcasted_iota(jnp.int32, (8, 256), 0)
    column = lax.broadcasted_iota(jnp.int32, (8, 256), 1)
    picks = [jnp.where(column == tile_ref[b] * 8 + row, 1.0, 0.0) for b in range(8)]
    pick = jnp.concatenate(picks, 0).astype(BF16)
    tf[:64, :] = dot(pick, wave[:256, :]).astype(BF16)
    tf[64:, :] = dot(pick, wave[256:, :]).astype(BF16)
    tft[...] = tf[...].astype(F32).T.astype(BF16)


def unpack_direction(dirg, d):
    for h in range(2):
        for q in range(4):
            for r in range(4):
                d[q, h, pl.ds(r, 64, stride=4), :] = dirg[h, pl.ds(r * 4 + q, 64, stride=16), :]

def map_rows(mv, g, k):
    v = mv[g, k].astype(F32)
    return v[0:1].reshape(8, 128), v[1:2].reshape(8, 128)

def forward_pass(mv, d, tf, tr, ti):
    def forward(i, carry):
        p, c = i // 8, i % 8
        re, im = [], []
        for h in range(2):
            cr, ci = [], []
            for g in range(32):
                mr, mi = map_rows(mv, g, c * 4 + p * 2 + h)
                dr = d[2 * p, h, g * 8:(g + 1) * 8, :]
                di = d[2 * p + 1, h, g * 8:(g + 1) * 8, :]
                cr.append(mr * dr - mi * di)
                ci.append(mr * di + mi * dr)
            re.append(jnp.concatenate(cr, 0).astype(BF16))
            im.append(jnp.concatenate(ci, 0).astype(BF16))
        t = dot(tf[:, :256], jnp.concatenate(re, 1)) + dot(tf[:, 256:], jnp.concatenate(im, 1))
        rows = pl.ds(pl.multiple_of(i * 64, 64), 64)
        tr[rows, :] = t[:64].astype(BF16)
        ti[rows, :] = t[64:].astype(BF16)
        return carry
    lax.fori_loop(0, 16, forward, 0, unroll=4)

def halves(ks, rows, re, im):
    for h in range(2):
        ks[0, h, rows, :] = re[:, h * 128:(h + 1) * 128]
        ks[1, h, rows, :] = im[:, h * 128:(h + 1) * 128]

def strided(ks, part, rows):
    return jnp.concatenate([ks[part, 0, rows, :], ks[part, 1, rows, :]], 1)

def row_pass(wave, a_ref, b_ref, ks, inverse):
    cosm, sinm, nsinm = wave[:256, :256], wave[:256, 256:], wave[256:, :256]
    s1, s2 = (nsinm, sinm) if inverse else (sinm, nsinm)
    def row(i, carry):
        rows = pl.ds(pl.multiple_of(i * 256, 256), 256)
        a, b = a_ref[rows, :], b_ref[rows, :]
        halves(ks, rows, dot(a, cosm) + dot(b, s1), dot(a, s2) + dot(b, cosm))
        return carry
    lax.fori_loop(0, 4, row, 0)

def sample_pass(ks, wv, gr, gi):
    def block(b, carry):
        parts = []
        for r in range(8):
            rows = pl.ds(b * 8 + r, 16, stride=64)
            parts.append(jnp.concatenate([strided(ks, 0, rows), strided(ks, 1, rows)], 0).astype(BF16))
        picked = jnp.concatenate(parts, 1)
        w = wv[b]
        s = dot(picked, w, (((1,), (1,)), ((), ()))).astype(BF16)
        g = dot(s, w).astype(BF16)
        for r in range(8):
            rows = pl.ds(pl.multiple_of((b * 8 + r) * 16, 16), 16)
            gr[rows, :] = g[:16, r * 256:(r + 1) * 256]
            gi[rows, :] = g[16:, r * 256:(r + 1) * 256]
        return carry
    lax.fori_loop(0, 8, block, 0, unroll=2)

def combine_pass(ks, tft, mv, acc, p):
    def combine(c, carry):
        i = p * 8 + c
        rows = pl.ds(i, 64, stride=16)
        sp = jnp.concatenate([strided(ks, 0, rows), strided(ks, 1, rows)], 0).astype(BF16)
        img = dot(tft[...], sp)
        for h in range(2):
            for g in range(32):
                mr, mi = map_rows(mv, g, c * 4 + p * 2 + h)
                ir = img[g * 8:(g + 1) * 8, h * 128:(h + 1) * 128]
                ii = img[256 + g * 8:256 + (g + 1) * 8, h * 128:(h + 1) * 128]
                acc[2 * p, h, g * 8:(g + 1) * 8, :] += mr * ir + mi * ii
                acc[2 * p + 1, h, g * 8:(g + 1) * 8, :] += mr * ii - mi * ir
        return carry
    lax.fori_loop(0, 8, combine, 0, unroll=4)


def solve_kernel(tile_ref, d_ref, r_ref, m_hbm, wave_hbm, w_hbm, applied_ref, coef_ref,
                 own, dirg, dirf, d, tf, tft, tr, ti, ks, gr, gi, acc, wv, mv, wave,
                 part, came, zsend, zcame, d8, r8, row, rows,
                 load_sem, gsend, grecv, psend, precv, zsend_sem, zrecv_sem, ssend, srecv):
    here = Place()
    coil, spoke, hi, z, sibling, other = here.coil, here.spoke, here.hi, here.z, here.sibling, here.other
    me = here.in_plane(0)

    def line(j):
        to = (z + j) % 8
        return to, (to % 4, spoke + 8 * (to // 4 - hi))

    def greet(j, carry):
        signal((coil, here.chip(j)))
        return carry

    def greet_line(j, carry):
        signal(line(j)[1])
        return carry

    lax.fori_loop(1, 16, greet, 0)
    lax.fori_loop(1, 8, greet_line, 0)
    signal((coil, sibling))
    loads = [pltpu.make_async_copy(wave_hbm, wave, load_sem.at[9])]
    loads += [
        pltpu.make_async_copy(m_hbm.at[:, y], mv.at[:, :, :, y * 128:(y + 1) * 128], load_sem.at[y])
        for y in range(8)
    ]
    loads.append(pltpu.make_async_copy(w_hbm, wv, load_sem.at[8]))
    for load in loads:
        load.start()
    for k in range(8):
        own[2 * k:2 * k + 2, :] = d_ref[k // 2, k % 2]
        d8[k % 2, 2 * (k // 2):2 * (k // 2) + 2, :] = d_ref[k // 2, k % 2]
        r8[k % 2, 2 * (k // 2):2 * (k // 2) + 2, :] = r_ref[k // 2, k % 2]
    dirg[spoke] = own[...]
    acc[...] = jnp.zeros_like(acc)
    pl.semaphore_wait(pltpu.get_barrier_semaphore(), 23)

    def send(src, slot, phase, j, device):
        return remote(src, dirg.at[slot], gsend.at[phase, j], grecv.at[slot], device)

    def arrived(slot):
        remote(own, dirg.at[slot], gsend.at[0, 0], grecv.at[slot], (coil, sibling)).wait_recv()

    send(own, spoke, 2, 0, (3 - coil, other)).start()

    def first(j, carry):
        send(own, spoke, 0, j, (coil, here.chip(j))).start()
        return carry

    lax.fori_loop(1, 16, first, 0)
    send(own, spoke, 0, 0, (coil, sibling)).start()
    loads[0].wait()
    tables(tile_ref, wave, tf, tft)
    arrived(other)

    def second(j, carry):
        send(dirg.at[other], other, 1, j, (coil, here.chip(j))).start()
        return carry

    lax.fori_loop(1, 16, second, 0)
    send(dirg.at[other], other, 1, 0, (coil, sibling)).start()
    flip = 8 - 16 * hi
    for phase, shift in ((2, 0), (3, flip)):
        def relay(j, carry, phase=phase, shift=shift):
            slot = here.chip(j) + shift
            arrived(slot)
            send(dirg.at[slot], slot, phase, j, (coil, sibling)).start()
            return carry

        lax.fori_loop(1, 16, relay, 0)

    def rest(j, carry):
        slot = here.chip(j) + 1 - 2 * here.core
        arrived(slot)
        arrived(slot + flip)
        return carry

    lax.fori_loop(0, 16, rest, 0)
    for h in range(2):
        dirf[h] = dirg[:, :, h * 128:(h + 1) * 128].reshape(1024, 128)
    unpack_direction(dirf, d)
    for load in loads[1:]:
        load.wait()
    forward_pass(mv, d, tf, tr, ti)
    row_pass(wave, tr, ti, ks, False)
    sample_pass(ks, wv, gr, gi)
    row_pass(wave, gr, gi, ks, True)

    def exchange(p, j):
        q = here.in_plane(j)
        return remote(part.at[p, q // 8, :, q % 8], came.at[p, me], psend.at[p, j], precv.at[p, me],
                      (coil, spoke_of(q, hi)))

    for p in range(2):
        combine_pass(ks, tft, mv, acc, p)
        for h in range(2):
            for k in range(2):
                for r in range(4):
                    dirf[h, pl.ds(r * 2 + k, 64, stride=8), :] = acc[2 * p + k, h, pl.ds(r, 64, stride=4), :]
            part[p, :, :, :, :, h * 128:(h + 1) * 128] = dirf[h, :512].astype(BF16).reshape(4, 2, 8, 8, 128)

        def start(j, carry, p=p):
            exchange(p, j).start()
            return carry

        lax.fori_loop(1, 32, start, 0)
        came[p, me] = part[p, here.y, :, here.x * 2 + here.core]

    def zcopy(p, j):
        to, device = line(j)
        return remote(zsend.at[p, to // 4], zcame.at[p, z], zsend_sem.at[p, j], zrecv_sem.at[p, z], device)

    for p in range(2):
        def came_in(j, carry, p=p):
            q = here.in_plane(j)
            remote(came.at[p, q], came.at[p, q], psend.at[p, j], precv.at[p, q], (coil, sibling)).wait_recv()
            return carry

        lax.fori_loop(1, 32, came_in, 0)
        total = came[p, 0].astype(F32)
        for q in range(1, 32):
            total = total + came[p, q].astype(F32)
        zsend[p] = total.astype(BF16)

        def zstart(j, carry, p=p):
            zcopy(p, j).start()
            return carry

        lax.fori_loop(1, 8, zstart, 0)
        zcame[p, z] = zsend[p, hi]

    applied = []
    sums = [0.0, 0.0, 0.0, 0.0]
    for p in range(2):
        def zwait(j, carry, p=p):
            frm = (z + j) % 8
            remote(zsend.at[p, 0], zcame.at[p, frm], zsend_sem.at[p, j], zrecv_sem.at[p, frm],
                   (coil, sibling)).wait_recv()
            return carry

        lax.fori_loop(1, 8, zwait, 0)
        value = zcame[p, 0].astype(F32)
        for k in range(1, 8):
            value = value + zcame[p, k].astype(F32)
        dp, rp = d8[p], r8[p]
        value = value + ridge * dp
        applied.append(value)
        for k, term in enumerate((rp * rp, dp * value, rp * value, value * value)):
            sums[k] = sums[k] + jnp.sum(term)
    lane = lax.broadcasted_iota(jnp.int32, (1, 128), 1)
    mine = jnp.zeros((1, 128), F32)
    for k in range(4):
        mine = jnp.where(lane == k, sums[k], mine)
    row[...] = mine
    rows[spoke] = mine

    def share(j):
        return remote(row, rows.at[spoke], ssend.at[j], srecv.at[spoke],
                      (coil, spoke_of(here.in_plane(j), hi)))

    def share_across(j):
        return remote(row, rows.at[spoke], ssend.at[32 + j], srecv.at[spoke],
                      (3 - coil, spoke_of(here.in_plane(j), 1 - hi)))

    def share_start(j, carry):
        share(j).start()
        return carry

    def across_start(j, carry):
        share_across(j).start()
        return carry

    lax.fori_loop(0, 32, across_start, 0)
    lax.fori_loop(1, 32, share_start, 0)
    for k in range(8):
        applied_ref[k // 2, k % 2] = applied[k % 2][2 * (k // 2):2 * (k // 2) + 2]

    def share_wait(j, carry):
        frm = (spoke + j) % 64
        remote(row, rows.at[frm], ssend.at[j], srecv.at[frm], (coil, sibling)).wait_recv()
        return carry

    lax.fori_loop(1, 64, share_wait, 0)
    total = jnp.sum(rows[...], axis=0)
    norm_now, curvature, crossing, squared = (
        jnp.sum(jnp.where(lane == k, total, 0.0), axis=1, keepdims=True) for k in range(4)
    )
    alpha = norm_now / curvature
    norm_next = norm_now - 2.0 * alpha * crossing + alpha * alpha * squared
    coef_ref[0:1, :] = jnp.broadcast_to(alpha, (1, 256))
    coef_ref[1:2, :] = jnp.broadcast_to(norm_next / norm_now, (1, 256))
    for phase in range(4):
        def gsent(j, carry, phase=phase):
            send(own, spoke, phase, j, (coil, sibling)).wait_send()
            return carry

        lax.fori_loop(1 if phase == 3 else 0, 16, gsent, 0)

    def sent(j, carry):
        exchange(0, j).wait_send()
        exchange(1, j).wait_send()
        share(j).wait_send()
        return carry

    def zsent(j, carry):
        zcopy(0, j).wait_send()
        zcopy(1, j).wait_send()
        return carry

    def across_sent(j, carry):
        share_across(j).wait_send()
        return carry

    lax.fori_loop(1, 32, sent, 0)
    lax.fori_loop(1, 8, zsent, 0)
    lax.fori_loop(0, 32, across_sent, 0)


def solve_call(tile_index, direction, residual, maps, wave, w):
    vm = pl.BlockSpec(memory_space=pltpu.VMEM)
    hbm = pl.BlockSpec(memory_space=pl.ANY)
    dma = pltpu.SemaphoreType.DMA
    return pl.pallas_call(
        solve_kernel,
        out_shape=(jax.ShapeDtypeStruct((4, 2, 2, 256), F32), jax.ShapeDtypeStruct((2, 256), F32)),
        in_specs=[pl.BlockSpec(memory_space=pltpu.SMEM), vm, vm, hbm, hbm, hbm],
        out_specs=(vm, vm),
        scratch_shapes=[
            pltpu.VMEM((16, 256), F32),
            pltpu.VMEM((64, 16, 256), F32),
            pltpu.VMEM((2, 1024, 128), F32),
            pltpu.VMEM((4, 2, 256, 128), F32),
            pltpu.VMEM((128, 512), BF16),
            pltpu.VMEM((512, 128), BF16),
            pltpu.VMEM((1024, 256), BF16),
            pltpu.VMEM((1024, 256), BF16),
            pltpu.VMEM((2, 2, 1024, 128), F32),
            pltpu.VMEM((1024, 256), BF16),
            pltpu.VMEM((1024, 256), BF16),
            pltpu.VMEM((4, 2, 256, 128), F32),
            pltpu.VMEM((8, 128, 2048), BF16),
            pltpu.VMEM((32, 32, 2, 1024), BF16),
            pltpu.VMEM((512, 512), BF16),
            pltpu.VMEM((2, 4, 2, 8, 8, 256), BF16),
            pltpu.VMEM((2, 32, 2, 8, 256), BF16),
            pltpu.VMEM((2, 2, 8, 256), BF16),
            pltpu.VMEM((2, 8, 8, 256), BF16),
            pltpu.VMEM((2, 8, 256), F32),
            pltpu.VMEM((2, 8, 256), F32),
            pltpu.VMEM((1, 128), F32),
            pltpu.VMEM((64, 1, 128), F32),
            dma((10,)), dma((4, 16)), dma((64,)), dma((2, 32)), dma((2, 32)),
            dma((2, 8)), dma((2, 8)), dma((64,)), dma((64,)),
        ],
        compiler_params=pltpu.CompilerParams(
            collective_id=0, has_side_effects=True, vmem_limit_bytes=60 * 2**20
        ),
        name="solve",
    )(tile_index, direction, residual, maps, wave, w)


def maps_view(maps):
    parts = maps.reshape(32, 8, 16, 2, 2, 128).transpose(0, 1, 2, 4, 3, 5)
    return parts.reshape(32, 8, 32, 2, 128)


def shards(image, residual, direction, coil_maps, interp_weights, tile_index):
    applied, coef = solve_call(
        tile_index, direction, residual, maps_view(coil_maps), jnp.asarray(wave_block()), interp_weights
    )
    new_residual = residual - coef[0] * applied
    new_image = image + coef[0] * direction
    new_direction = new_residual + coef[1] * direction
    return (new_image, new_residual, new_direction)


def solution(mesh):
    rows = P("spoke", None, None, None)
    in_specs = (rows, rows, rows, P(None, "coil", None, None, None), P("spoke", None, None), P("spoke"))
    return jax.shard_map(shards, mesh=mesh, in_specs=in_specs, out_specs=(rows, rows, rows), check_vma=False)
```

profile of v0, /device:TPU:1, one launch (start us, length us, event | category | flops | bytes accessed | tf_op | source)
XLA Modules:
  0.0 62.6 jit_solution(9095487561170568204)
XLA Ops:
  0.6 0.0 copy-start
  0.6 0.0 copy-start.1
  0.7 0.0 copy-start.2
  0.7 59.8 %solve.1 = (f32[4,2,2,256]{3,2,1,0:T(2,128)}, f32[2,256]{1,0:T(2,128)}) custom-call(s32[8]{0:T(128)} %tile_ref.1, f32[4,2,2,256]{3,2,1,0:T(2,128)} %d_ref.1, f32[4,2,2,256]{3,2,1,0:T(2,128)} %r_ref.1, bf16[32,8,32,2,128]{4,3,2,1,0:T(2,128)(2,1)} %bitcast.7, bf16[512,512]{1,0:T(8,128)(2,1)} %constant.2.clone.wave_hbm, bf16[8,128,2048]{2,1,0:T(8,128)(2,1)} %w_hbm.1), custom_call_target="tpu_custom_call" | custom-call | tf_op jit(solution)/shard_map/solve/pallas_call | solution.py:379
  60.4 0.8 %fusion = (f32[1,256]{1,0:T(1,128)S(1)}, f32[1,256]{1,0:T(1,128)S(1)}) fusion(f32[2,256]{1,0:T(2,128)} %get-tuple-element.5), kind=kLoop, calls=%fused_computation.3 | loop fusion | bytes 4096 | tf_op jit(solution)/shard_map/slice | solution.py:429
  61.2 0.0 copy-done
  61.2 0.0 copy-done.1
  61.2 0.0 copy-done.2
  61.2 1.4 %multiply_add_fusion = (f32[4,2,2,256]{3,2,1,0:T(2,128)}, f32[4,2,2,256]{3,2,1,0:T(2,128)}, f32[4,2,2,256]{3,2,1,0:T(2,128)}) fusion(f32[4,2,2,256]{3,2,1,0:T(2,128)S(1)} %copy-done, f32[256]{0:T(256)S(1)} %bitcast.8, f32[4,2,2,256]{3,2,1,0:T(2,128)S(1)} %copy-done.1, f32[4,2,2,256]{3,2,1,0:T(2,128)} %get-tuple-element.6, f32[256]{0:T(256)S(1)} %bitcast.9, ...), kind=kLoop, calls=%fused_computation | loop fusion | flops 24576 | bytes 116736 | tf_op jit(solution)/shard_map/add | solution.py:429
Async XLA Ops:
  0.6 60.6 %copy-start = (f32[4,2,2,256]{3,2,1,0:T(2,128)S(1)}, f32[4,2,2,256]{3,2,1,0:T(2,128)}, u32[]{:S(2)}) copy-start(f32[4,2,2,256]{3,2,1,0:T(2,128)} %d_ref.1) | copy-start | bytes 49156
  0.6 60.5 %copy-start.1 = (f32[4,2,2,256]{3,2,1,0:T(2,128)S(1)}, f32[4,2,2,256]{3,2,1,0:T(2,128)}, u32[]{:S(2)}) copy-start(f32[4,2,2,256]{3,2,1,0:T(2,128)} %r_ref.1) | copy-start | bytes 49156
  0.7 60.5 %copy-start.2 = (f32[4,2,2,256]{3,2,1,0:T(2,128)S(1)}, f32[4,2,2,256]{3,2,1,0:T(2,128)}, u32[]{:S(2)}) copy-start(f32[4,2,2,256]{3,2,1,0:T(2,128)} %param.7) | copy-start | bytes 49156
where the time goes:
time: 62.9 us; the launch traced here: 62.6 us
  Pallas kernels  59.8 us (95%)
  other arithmetic  1.36 us (2%)
  local copies, waits for them, and re-layouts  0.77 us (1%)
  between operations  0.68 us (1%)
    pallas_call x1, Pallas kernels, solve_call(): pl.pallas_call(solve_kernel, out_shape=(jax.ShapeDtypeStruct((4, 2, 2, 25...  59.8 us
    add x1, other arithmetic, shards(): new_direction = new_residual + coef[1] * direction  1.36 us

commit v1 on v0

v1 whole, which is shorter than its diff:
```python
import math

import jax
import jax.numpy as jnp
import numpy as np
from jax import lax
from jax.experimental import pallas as pl
from jax.experimental.pallas import tpu as pltpu
from jax.sharding import PartitionSpec as P

F32, BF16 = jnp.float32, jnp.bfloat16
MESH = pl.DeviceIdType.MESH
NT = (((1,), (1,)), ((), ()))
ridge = 0.1
RING = (2, 1, 3, 0)
STEPS = sorted(((j, i) for j in range(4) for i in range(4)), key=lambda s: -min(s[0], 4 - s[0]) - min(s[1], 4 - s[1]))


class Place:
    def __init__(self):
        self.coil = lax.axis_index("coil")
        self.spoke = lax.axis_index("spoke")
        self.core = self.spoke % 2
        x = (self.spoke // 2) % 4
        self.hi = (self.spoke // 8) % 2
        y = self.spoke // 16
        self.z = self.hi * 4 + self.coil
        self.sibling = self.spoke + 1 - 2 * self.core
        self.flip = 8 - 16 * self.hi
        self.ys = [(y + j) % 4 for j in range(4)]
        self.xs = [((x + j) % 4) * 2 for j in range(4)]
        self.cores = [self.core, 1 - self.core]
        self.rows = [v * 16 + self.hi * 8 for v in self.ys]

    def chip(self, step):
        return self.rows[step[0]] + self.xs[step[1]] + self.core

    def line(self, j):
        to = (self.z + j) % 8
        return to // 4, (to % 4, self.spoke + 8 * (to // 4 - self.hi))


def signal(device):
    pl.semaphore_signal(pltpu.get_barrier_semaphore(), inc=1, device_id=device, device_id_type=MESH)


def remote(src, dst, send_sem, recv_sem, device):
    return pltpu.make_async_remote_copy(
        src_ref=src, dst_ref=dst, send_sem=send_sem, recv_sem=recv_sem,
        device_id=device, device_id_type=MESH,
    )


def wave_block():
    n = 256
    q = (np.arange(n)[:, None] * np.arange(n)[None, :]) % n
    ang = q.astype(np.float32) * np.float32(2.0 * math.pi / n)
    c = (np.cos(ang) * np.float32(1.0 / math.sqrt(n))).astype(jnp.bfloat16)
    s = (np.sin(ang) * np.float32(1.0 / math.sqrt(n))).astype(jnp.bfloat16)
    return np.concatenate([np.concatenate([c, s], 1), np.concatenate([-s, c], 1)], 0)


def wave_columns():
    return np.arange(512).reshape(2, 4, 2, 32).transpose(2, 0, 1, 3).reshape(-1)


def dot(a, b, dims=(((1,), (0,)), ((), ()))):
    return lax.dot_general(a, b, dims, preferred_element_type=F32)


def tables(tile_ref, wave, tf, tft):
    row = lax.broadcasted_iota(jnp.int32, (8, 256), 0)
    column = lax.broadcasted_iota(jnp.int32, (8, 256), 1)
    picks = [jnp.where(column == tile_ref[b] * 8 + row, 1.0, 0.0) for b in range(8)]
    pick = jnp.concatenate(picks, 0).astype(BF16)
    tf[:64, :] = dot(pick, wave[:256, :]).astype(BF16)
    tf[64:, :] = dot(pick, wave[256:, :]).astype(BF16)
    tft[...] = tf[...].astype(F32).T.astype(BF16)


def unpack_direction(dirg, d, side):
    for y in range(4):
        base = pl.multiple_of((y * 2 + side) * 256, 256)
        for h in range(2):
            for q in range(4):
                for r in range(4):
                    d[q, h, pl.ds(y * 32 + r, 8, stride=4), :] = dirg[pl.ds(base + h * 16 + r * 4 + q, 8, stride=32), :]


def map_rows(mv, g, k):
    v = mv[g, k].astype(F32)
    return v[0:1].reshape(8, 128), v[1:2].reshape(8, 128)


def forward_terms(mv, d, tf, side, i):
    p, c = i // 8, i % 8
    re, im = [], []
    for h in range(2):
        cr, ci = [], []
        for g in range(16):
            mr, mi = map_rows(mv, (g // 4) * 8 + side * 4 + g % 4, c * 4 + p * 2 + h)
            dr = d[2 * p, h, g * 8:(g + 1) * 8, :]
            di = d[2 * p + 1, h, g * 8:(g + 1) * 8, :]
            cr.append(mr * dr - mi * di)
            ci.append(mr * di + mi * dr)
        re.append(jnp.concatenate(cr, 0).astype(BF16))
        im.append(jnp.concatenate(ci, 0).astype(BF16))
    coil = jnp.concatenate([jnp.concatenate(re, 1), jnp.concatenate(im, 1)], 0)
    return dot(tf[:, pl.ds(pl.multiple_of(side * 256, 256), 256)], coil)


def halves(ks, rows, re, im):
    for h in range(2):
        ks[0, h, rows, :] = re[:, h * 128:(h + 1) * 128]
        ks[1, h, rows, :] = im[:, h * 128:(h + 1) * 128]


def strided(ks, part, rows):
    return jnp.concatenate([ks[part, 0, rows, :], ks[part, 1, rows, :]], 1)


def row_pass(wave, a_ref, b_ref, ks, inverse):
    cosm, sinm, nsinm = wave[:256, :256], wave[:256, 256:], wave[256:, :256]
    s1, s2 = (nsinm, sinm) if inverse else (sinm, nsinm)
    for i in range(4):
        rows = pl.ds(i * 256, 256)
        a, b = a_ref[rows, :], b_ref[rows, :]
        halves(ks, rows, dot(a, cosm) + dot(b, s1), dot(a, s2) + dot(b, cosm))


def sample_pass(ks, wv, gr, gi):
    samples = []
    for b in range(8):
        parts = []
        for r in range(8):
            rows = pl.ds(b * 8 + r, 16, stride=64)
            parts.append(jnp.concatenate([strided(ks, 0, rows), strided(ks, 1, rows)], 0).astype(BF16))
        samples.append(dot(jnp.concatenate(parts, 1), wv[b], NT).astype(BF16))
    for b in range(8):
        g = dot(samples[b], wv[b]).astype(BF16)
        for r in range(8):
            rows = pl.ds((b * 8 + r) * 16, 16)
            gr[rows, :] = g[:16, r * 256:(r + 1) * 256]
            gi[rows, :] = g[16:, r * 256:(r + 1) * 256]


def spread_pass(ks, sp):
    for i in range(16):
        rows = pl.ds(i, 64, stride=16)
        sp[i] = jnp.concatenate([strided(ks, 0, rows), strided(ks, 1, rows)], 0).astype(BF16)


def combine_rows(sp, tft, mv, acc, stage, part, y):
    table = jnp.concatenate(
        [tft[pl.ds(pl.multiple_of(s * 256 + k * 128 + y * 32, 32), 32), :] for k in range(2) for s in range(2)], 0
    )

    def plane(p, carry):
        re = [[None] * 8, [None] * 8]
        im = [[None] * 8, [None] * 8]
        for c in range(8):
            img = dot(table, sp[p * 8 + c])
            for h in range(2):
                for g in range(8):
                    mr, mi = map_rows(mv, y * 8 + g, c * 4 + p * 2 + h)
                    ir = img[g * 8:(g + 1) * 8, h * 128:(h + 1) * 128]
                    ii = img[64 + g * 8:64 + (g + 1) * 8, h * 128:(h + 1) * 128]
                    a, b = mr * ir + mi * ii, mr * ii - mi * ir
                    re[h][g] = a if c == 0 else re[h][g] + a
                    im[h][g] = b if c == 0 else im[h][g] + b
        for h in range(2):
            acc[0, h] = jnp.concatenate(re[h], 0)
            acc[1, h] = jnp.concatenate(im[h], 0)
            for s in range(2):
                for k in range(2):
                    for r in range(4):
                        stage[h, pl.ds(s * 8 + k * 4 + r, 8, stride=16), :] = acc[k, h, pl.ds(s * 32 + r, 8, stride=4), :]
            part[y, :, p, :, :, h * 128:(h + 1) * 128] = stage[h].astype(BF16).reshape(8, 2, 8, 128)
        return carry

    lax.fori_loop(0, 2, plane, 0)


def solve_kernel(tile_ref, d_hbm, r_hbm, m_hbm, wave_hbm, wavep_hbm, w_hbm, applied_ref, alpha_ref, beta_ref,
                 dv, rv, own, dirg, d, tf, tft, tacc, tr, ti, ks, gr, gi, sp, acc, stage, wv, mv, wave, wavep,
                 part, came, zsend, zcame, d8, r8, row, rows,
                 load_sem, gsend, grecv, brecv, psend, precv, zsend_sem, zrecv_sem, ssend, srecv):
    here = Place()
    coil, spoke, hi, z, sibling = here.coil, here.spoke, here.hi, here.z, here.sibling
    other = spoke + here.flip
    near = [pltpu.make_async_copy(d_hbm, dv, load_sem.at[9]), pltpu.make_async_copy(r_hbm, rv, load_sem.at[10])]
    for load in near:
        load.start()
    for step in STEPS[:15]:
        signal((coil, here.chip(step)))
    for j in (4, 3, 5, 2, 6, 1, 7):
        signal(here.line(j)[1])
    signal((coil, sibling))
    loads = [pltpu.make_async_copy(wavep_hbm, wavep, load_sem.at[11]), pltpu.make_async_copy(wave_hbm, wave, load_sem.at[12])]
    loads += [
        pltpu.make_async_copy(m_hbm.at[:, y], mv.at[:, :, :, y * 128:(y + 1) * 128], load_sem.at[y])
        for y in range(8)
    ]
    loads.append(pltpu.make_async_copy(w_hbm, wv, load_sem.at[8]))
    for load in near:
        load.wait()
    for load in loads:
        load.start()
    for r in range(4):
        for p in range(2):
            for h in range(2):
                own[h * 16 + r * 4 + p * 2:h * 16 + r * 4 + p * 2 + 2, :] = dv[r, p, :, h * 128:(h + 1) * 128]
            for k in range(2):
                d8[p, k * 4 + r:k * 4 + r + 1, :] = dv[r, p, k:k + 1, :]
                r8[p, k * 4 + r:k * 4 + r + 1, :] = rv[r, p, k:k + 1, :]

    def slot(s):
        return dirg.at[pl.ds(pl.multiple_of(s * 32, 32), 32)]

    dirg[pl.ds(pl.multiple_of(spoke * 32, 32), 32), :] = own[...]
    pl.semaphore_wait(pltpu.get_barrier_semaphore(), 23)

    def send(src, s, device, recv_sem):
        remote(src, slot(s), gsend, recv_sem, device).start()

    def arrived(s):
        remote(own, slot(s), gsend, grecv.at[s], (coil, sibling)).wait_recv()

    def relayed(k):
        sixteen = dirg.at[pl.ds(0, 512)]
        remote(sixteen, sixteen, gsend, brecv.at[k], (coil, sibling)).wait_recv()

    send(own, spoke, (3 - coil, other), grecv.at[spoke])
    for step in STEPS[:15]:
        send(own, spoke, (coil, here.chip(step)), grecv.at[spoke])
    send(own, spoke, (coil, sibling), brecv.at[0])
    loads[0].wait()
    tables(tile_ref, wavep, tf, tft)
    arrived(other)
    for step in STEPS[:15]:
        send(slot(other), other, (coil, here.chip(step)), grecv.at[other])
    send(slot(other), other, (coil, sibling), brecv.at[1])
    for step in STEPS[:15]:
        s = here.chip(step)
        arrived(s)
        send(slot(s), s, (coil, sibling), brecv.at[0])
    relayed(0)
    unpack_direction(dirg, d, hi)
    for load in loads[1:10]:
        load.wait()
    for k in range(4):
        def first_half(i, carry):
            tacc[i] = forward_terms(mv, d, tf, hi, i)
            return carry

        lax.fori_loop(4 * k, 4 * k + 4, first_half, 0, unroll=4)
        for step in STEPS[4 * k:min(4 * k + 4, 15)]:
            s = here.chip(step) + here.flip
            arrived(s)
            send(slot(s), s, (coil, sibling), brecv.at[1])
    relayed(1)
    unpack_direction(dirg, d, 1 - hi)

    def second_half(i, carry):
        t = tacc[i] + forward_terms(mv, d, tf, 1 - hi, i)
        where = pl.ds(pl.multiple_of(i * 64, 64), 64)
        tr[where, :] = t[:64].astype(BF16)
        ti[where, :] = t[64:].astype(BF16)
        return carry

    lax.fori_loop(0, 16, second_half, 0, unroll=4)
    row_pass(wave, tr, ti, ks, False)
    loads[10].wait()
    sample_pass(ks, wv, gr, gi)
    row_pass(wave, gr, gi, ks, True)
    spread_pass(ks, sp)
    me = here.ys[0] * 8 + here.xs[0] + here.core
    for j in RING:
        y = here.ys[j]
        combine_rows(sp, tft, mv, acc, stage, part, y)
        for i in RING:
            for k in (1, 0):
                if (j, i, k) == (0, 0, 0):
                    continue
                xc = here.xs[i] + here.cores[k]
                remote(part.at[y, xc], came.at[me], psend, precv, (coil, here.rows[j] + xc)).start()
    came[me] = part[here.ys[0], here.xs[0] + here.core]
    dirgs = dirg.at[pl.ds(0, 63 * 32)]
    remote(dirgs, dirgs, gsend, brecv.at[0], (coil, sibling)).wait_send()
    others = came.at[pl.ds(0, 31)]
    remote(others, others, psend, precv, (coil, sibling)).wait_recv()
    for p in range(2):
        for s in range(2):
            total = came[0, p, s].astype(F32)
            for q in range(1, 32):
                total = total + came[q, p, s].astype(F32)
            zsend[s, p] = total.astype(BF16)
    for j in (4, 3, 5, 2, 6, 1, 7):
        s, device = here.line(j)
        remote(zsend.at[s], zcame.at[z], zsend_sem, zrecv_sem, device).start()
    zcame[z] = zsend[hi]
    remote(others, others, psend, precv, (coil, sibling)).wait_send()
    seven = zcame.at[pl.ds(0, 7)]
    remote(seven, seven, zsend_sem, zrecv_sem, (coil, sibling)).wait_recv()
    applied = []
    sums = [0.0, 0.0, 0.0, 0.0]
    for p in range(2):
        value = zcame[0, p].astype(F32)
        for k in range(1, 8):
            value = value + zcame[k, p].astype(F32)
        dp, rp = d8[p], r8[p]
        value = value + ridge * dp
        applied.append(value)
        for k, term in enumerate((rp * rp, dp * value, rp * value, value * value)):
            sums[k] = sums[k] + jnp.sum(term)
    lane = lax.broadcasted_iota(jnp.int32, (1, 128), 1)
    mine = jnp.zeros((1, 128), F32)
    for k in range(4):
        mine = jnp.where(lane == k, sums[k], mine)
    row[...] = mine
    rows[spoke] = mine
    for across in (1, 0):
        for j, i in STEPS:
            for k in (1, 0):
                if (across, j, i, k) == (0, 0, 0, 0):
                    continue
                to = here.rows[j] + here.xs[i] + here.cores[k] + across * here.flip
                where = 3 - coil if across else coil
                remote(row, rows.at[spoke], ssend, srecv, (where, to)).start()
    for r in range(4):
        for p in range(2):
            for k in range(2):
                applied_ref[r, p, k:k + 1, :] = applied[p][k * 4 + r:k * 4 + r + 1, :]
    remote(seven, seven, zsend_sem, zrecv_sem, (coil, sibling)).wait_send()
    most = rows.at[pl.ds(0, 63)]
    remote(most, most, ssend, srecv, (coil, sibling)).wait_recv()
    total = jnp.sum(rows[...], axis=0)
    norm_now, curvature, crossing, squared = (
        jnp.sum(jnp.where(lane == k, total, 0.0), axis=1, keepdims=True) for k in range(4)
    )
    alpha = norm_now / curvature
    norm_next = norm_now - 2.0 * alpha * crossing + alpha * alpha * squared
    alpha, beta = (jnp.broadcast_to(v, (2, 256)) for v in (alpha, norm_next / norm_now))
    for r in range(4):
        for p in range(2):
            alpha_ref[r, p] = alpha
            beta_ref[r, p] = beta
    remote(most, most, ssend, srecv, (coil, sibling)).wait_send()


def solve_call(tile_index, direction, residual, maps, wave, wavep, w):
    vm = pl.BlockSpec(memory_space=pltpu.VMEM)
    hbm = pl.BlockSpec(memory_space=pl.ANY)
    dma = pltpu.SemaphoreType.DMA
    block = jax.ShapeDtypeStruct((4, 2, 2, 256), F32)
    return pl.pallas_call(
        solve_kernel,
        out_shape=(block, block, block),
        in_specs=[pl.BlockSpec(memory_space=pltpu.SMEM)] + [hbm] * 6,
        out_specs=(vm, vm, vm),
        scratch_shapes=[
            pltpu.VMEM((4, 2, 2, 256), F32),
            pltpu.VMEM((4, 2, 2, 256), F32),
            pltpu.VMEM((32, 128), F32),
            pltpu.VMEM((2048, 128), F32),
            pltpu.VMEM((4, 2, 128, 128), F32),
            pltpu.VMEM((128, 512), BF16),
            pltpu.VMEM((512, 128), BF16),
            pltpu.VMEM((16, 128, 256), F32),
            pltpu.VMEM((1024, 256), BF16),
            pltpu.VMEM((1024, 256), BF16),
            pltpu.VMEM((2, 2, 1024, 128), F32),
            pltpu.VMEM((1024, 256), BF16),
            pltpu.VMEM((1024, 256), BF16),
            pltpu.VMEM((16, 128, 256), BF16),
            pltpu.VMEM((2, 2, 64, 128), F32),
            pltpu.VMEM((2, 128, 128), F32),
            pltpu.VMEM((8, 128, 2048), BF16),
            pltpu.VMEM((32, 32, 2, 1024), BF16),
            pltpu.VMEM((512, 512), BF16),
            pltpu.VMEM((512, 512), BF16),
            pltpu.VMEM((4, 8, 2, 2, 8, 256), BF16),
            pltpu.VMEM((32, 2, 2, 8, 256), BF16),
            pltpu.VMEM((2, 2, 8, 256), BF16),
            pltpu.VMEM((8, 2, 8, 256), BF16),
            pltpu.VMEM((2, 8, 256), F32),
            pltpu.VMEM((2, 8, 256), F32),
            pltpu.VMEM((1, 128), F32),
            pltpu.VMEM((64, 1, 128), F32),
            dma((13,)), dma, dma((64,)), dma((2,)), dma, dma, dma, dma, dma, dma,
        ],
        compiler_params=pltpu.CompilerParams(
            collective_id=0, has_side_effects=True, vmem_limit_bytes=60 * 2**20
        ),
        name="solve",
    )(tile_index, direction, residual, maps, wave, wavep, w)


def maps_view(maps):
    parts = maps.reshape(32, 8, 16, 2, 2, 128).transpose(0, 1, 2, 4, 3, 5)
    return parts.reshape(32, 8, 32, 2, 128)


def shards(image, residual, direction, coil_maps, interp_weights, tile_index):
    wave = wave_block()
    applied, alpha, beta = solve_call(
        tile_index, direction, residual, maps_view(coil_maps), jnp.asarray(wave),
        jnp.asarray(wave[:, wave_columns()]), interp_weights
    )
    new_residual = residual - alpha * applied
    new_image = image + alpha * direction
    new_direction = new_residual + beta * direction
    return (new_image, new_residual, new_direction)


def solution(mesh):
    rows = P("spoke", None, None, None)
    in_specs = (rows, rows, rows, P(None, "coil", None, None, None), P("spoke", None, None), P("spoke"))
    return jax.shard_map(shards, mesh=mesh, in_specs=in_specs, out_specs=(rows, rows, rows), check_vma=False)
```

time: 62.9 us -> 51.5 us (0.82)
  Pallas kernels: 59.8 us -> 49 us
  local copies, waits for them, and re-layouts: 0.77 us -> 0.01 us
    pallas_call x1, Pallas kernels: 59.8 us -> 49 us  [solve_call(): pl.pallas_call(solve_kernel, out_shape=(block, block, block), in_specs=[p...]
    slice x1 -> x0, local copies, waits for them, and re-layouts: 0.76 us -> none  [shards(): new_direction = new_residual + coef[1] * direction]
where the time goes in v1:
time: 51.5 us; the launch traced here: 51.1 us
  Pallas kernels  49 us (95%)
  other arithmetic  1.4 us (3%)
  between operations  0.69 us (1%)
    pallas_call x1, Pallas kernels, solve_call(): pl.pallas_call(solve_kernel, out_shape=(block, block, block), in_specs=[p...  49 us
    add x1, other arithmetic, shards(): new_direction = new_residual + beta * direction  1.4 us

profile of v1, /device:TPU:1, one launch (start us, length us, event | category | flops | bytes accessed | tf_op | source)
XLA Modules:
  0.0 51.1 jit_solution(6805478910425030186)
XLA Ops:
  0.6 0.0 copy-start
  0.6 0.0 copy-start.1
  0.7 0.0 copy-start.2
  0.7 49.0 %solve.1 = (f32[4,2,2,256]{3,2,1,0:T(2,128)}, f32[4,2,2,256]{3,2,1,0:T(2,128)}, f32[4,2,2,256]{3,2,1,0:T(2,128)}) custom-call(s32[8]{0:T(128)} %tile_ref.1, f32[4,2,2,256]{3,2,1,0:T(2,128)} %d_hbm.1, f32[4,2,2,256]{3,2,1,0:T(2,128)} %r_hbm.1, bf16[32,8,32,2,128]{4,3,2,1,0:T(2,128)(2,1)} %bitcast.5, bf16[512,512]{1,0:T(8,128)(2,1)} %constant.4.clone.wave_hbm, ...), custom_call_target="tpu_custom_call" | custom-call | tf_op jit(solution)/shard_map/solve/pallas_call | solution.py:356
  49.7 0.0 copy-done
  49.7 0.0 copy-done.1
  49.7 0.0 copy-done.2
  49.7 1.4 %multiply_add_fusion = (f32[4,2,2,256]{3,2,1,0:T(2,128)}, f32[4,2,2,256]{3,2,1,0:T(2,128)}, f32[4,2,2,256]{3,2,1,0:T(2,128)}) fusion(f32[4,2,2,256]{3,2,1,0:T(2,128)} %get-tuple-element.8, f32[4,2,2,256]{3,2,1,0:T(2,128)S(1)} %copy-done, f32[4,2,2,256]{3,2,1,0:T(2,128)S(1)} %copy-done.1, f32[4,2,2,256]{3,2,1,0:T(2,128)} %get-tuple-element.6, ...), kind=kLoop, calls=%fused_computation | loop fusion | flops 24576 | bytes 147456 | tf_op jit(solution)/shard_map/add | solution.py:412
Async XLA Ops:
  0.6 49.0 %copy-start = (f32[4,2,2,256]{3,2,1,0:T(2,128)S(1)}, f32[4,2,2,256]{3,2,1,0:T(2,128)}, u32[]{:S(2)}) copy-start(f32[4,2,2,256]{3,2,1,0:T(2,128)} %d_hbm.1) | copy-start | bytes 49156
  0.6 49.0 %copy-start.1 = (f32[4,2,2,256]{3,2,1,0:T(2,128)S(1)}, f32[4,2,2,256]{3,2,1,0:T(2,128)}, u32[]{:S(2)}) copy-start(f32[4,2,2,256]{3,2,1,0:T(2,128)} %r_hbm.1) | copy-start | bytes 49156
  0.7 49.0 %copy-start.2 = (f32[4,2,2,256]{3,2,1,0:T(2,128)S(1)}, f32[4,2,2,256]{3,2,1,0:T(2,128)}, u32[]{:S(2)}) copy-start(f32[4,2,2,256]{3,2,1,0:T(2,128)} %param.8) | copy-start | bytes 49156

commit v2 on v1

--- a/solution.py
+++ b/solution.py
@@ -80,11 +80,11 @@
 
 def unpack_direction(dirg, d, side):
     for y in range(4):
-        base = pl.multiple_of((y * 2 + side) * 256, 256)
+        base = (y * 2 + side) * 320
         for h in range(2):
             for q in range(4):
                 for r in range(4):
-                    d[q, h, pl.ds(y * 32 + r, 8, stride=4), :] = dirg[pl.ds(base + h * 16 + r * 4 + q, 8, stride=32), :]
+                    d[q, h, pl.ds(y * 32 + r, 8, stride=4), :] = dirg[pl.ds(base + h * 16 + r * 4 + q, 8, stride=40), :]
 
 
 def map_rows(mv, g, k):
@@ -125,7 +125,11 @@
     for i in range(4):
         rows = pl.ds(i * 256, 256)
         a, b = a_ref[rows, :], b_ref[rows, :]
-        halves(ks, rows, dot(a, cosm) + dot(b, s1), dot(a, s2) + dot(b, cosm))
+        re, im = dot(a, cosm) + dot(b, s1), dot(a, s2) + dot(b, cosm)
+        size = 16 if inverse else 64
+        for k in range(256 // size):
+            cut = slice(k * size, (k + 1) * size)
+            halves(ks, pl.ds((i * 256 // size + k) * (size + 8), size), re[cut], im[cut])
 
 
 def sample_pass(ks, wv, gr, gi):
@@ -133,7 +137,7 @@
     for b in range(8):
         parts = []
         for r in range(8):
-            rows = pl.ds(b * 8 + r, 16, stride=64)
+            rows = pl.ds(b * 8 + r, 16, stride=72)
             parts.append(jnp.concatenate([strided(ks, 0, rows), strided(ks, 1, rows)], 0).astype(BF16))
         samples.append(dot(jnp.concatenate(parts, 1), wv[b], NT).astype(BF16))
     for b in range(8):
@@ -146,7 +150,7 @@
 
 def spread_pass(ks, sp):
     for i in range(16):
-        rows = pl.ds(i, 64, stride=16)
+        rows = pl.ds(i, 64, stride=24)
         sp[i] = jnp.concatenate([strided(ks, 0, rows), strided(ks, 1, rows)], 0).astype(BF16)
 
 
@@ -174,21 +178,23 @@
             for s in range(2):
                 for k in range(2):
                     for r in range(4):
-                        stage[h, pl.ds(s * 8 + k * 4 + r, 8, stride=16), :] = acc[k, h, pl.ds(s * 32 + r, 8, stride=4), :]
-            part[y, :, p, :, :, h * 128:(h + 1) * 128] = stage[h].astype(BF16).reshape(8, 2, 8, 128)
+                        stage[h, pl.ds(s * 8 + k * 4 + r, 8, stride=24), :] = acc[k, h, pl.ds(s * 32 + r, 8, stride=4), :]
+            dense = jnp.concatenate([stage[h, i * 24:i * 24 + 16, :] for i in range(8)], 0)
+            part[y, :, :, p, :, :, h * 128:(h + 1) * 128] = dense.astype(BF16).reshape(4, 2, 2, 8, 128)
         return carry
 
     lax.fori_loop(0, 2, plane, 0)
 
 
-def solve_kernel(tile_ref, d_hbm, r_hbm, m_hbm, wave_hbm, wavep_hbm, w_hbm, applied_ref, alpha_ref, beta_ref,
-                 dv, rv, own, dirg, d, tf, tft, tacc, tr, ti, ks, gr, gi, sp, acc, stage, wv, mv, wave, wavep,
-                 part, came, zsend, zcame, d8, r8, row, rows,
-                 load_sem, gsend, grecv, brecv, psend, precv, zsend_sem, zrecv_sem, ssend, srecv):
+def solve_kernel(tile_hbm, d_hbm, r_hbm, m_hbm, wave_hbm, wavep_hbm, w_hbm, applied_ref, alpha_ref, beta_ref,
+                 tile_ref, dv, rv, own, dirg, d, tf, tft, tacc, tr, ti, ks, gr, gi, sp, acc, stage, wv, mv, wave, wavep,
+                 part, half, pair, came, zsend, zcame, d8, r8, row, rows,
+                 load_sem, gsend, grecv, brecv, asend, hsend, hrecv, psend, precv, zsend_sem, zrecv_sem, ssend, srecv, esend):
     here = Place()
     coil, spoke, hi, z, sibling = here.coil, here.spoke, here.hi, here.z, here.sibling
     other = spoke + here.flip
     near = [pltpu.make_async_copy(d_hbm, dv, load_sem.at[9]), pltpu.make_async_copy(r_hbm, rv, load_sem.at[10])]
+    near.append(pltpu.make_async_copy(tile_hbm, tile_ref, load_sem.at[13]))
     for load in near:
         load.start()
     for step in STEPS[:15]:
@@ -215,9 +221,9 @@
                 r8[p, k * 4 + r:k * 4 + r + 1, :] = rv[r, p, k:k + 1, :]
 
     def slot(s):
-        return dirg.at[pl.ds(pl.multiple_of(s * 32, 32), 32)]
-
-    dirg[pl.ds(pl.multiple_of(spoke * 32, 32), 32), :] = own[...]
+        return dirg.at[pl.ds(pl.multiple_of(s * 40, 8), 32)]
+
+    dirg[pl.ds(pl.multiple_of(spoke * 40, 8), 32), :] = own[...]
     pl.semaphore_wait(pltpu.get_barrier_semaphore(), 23)
 
     def send(src, s, device, recv_sem):
@@ -230,16 +236,23 @@
         sixteen = dirg.at[pl.ds(0, 512)]
         remote(sixteen, sixteen, gsend, brecv.at[k], (coil, sibling)).wait_recv()
 
-    send(own, spoke, (3 - coil, other), grecv.at[spoke])
+    edge = coil % 3 == 0
+    nearest = (3 - coil, 2 - coil // 3)
+
+    @pl.when(edge)
+    def _():
+        for to in nearest:
+            remote(own, slot(spoke), asend, grecv.at[spoke], (to, other)).start()
+
     for step in STEPS[:15]:
         send(own, spoke, (coil, here.chip(step)), grecv.at[spoke])
     send(own, spoke, (coil, sibling), brecv.at[0])
     loads[0].wait()
     tables(tile_ref, wavep, tf, tft)
     arrived(other)
+    send(slot(other), other, (coil, sibling), brecv.at[1])
     for step in STEPS[:15]:
         send(slot(other), other, (coil, here.chip(step)), grecv.at[other])
-    send(slot(other), other, (coil, sibling), brecv.at[1])
     for step in STEPS[:15]:
         s = here.chip(step)
         arrived(s)
@@ -274,25 +287,47 @@
     sample_pass(ks, wv, gr, gi)
     row_pass(wave, gr, gi, ks, True)
     spread_pass(ks, sp)
-    me = here.ys[0] * 8 + here.xs[0] + here.core
-    for j in RING:
+    core, mine_x = here.core, here.xs[0] // 2
+
+    def swap(k, y):
+        return remote(part.at[y, :, 1 - core], half.at[k], hsend, hrecv.at[k], (coil, sibling))
+
+    for k, j in enumerate(RING):
         y = here.ys[j]
         combine_rows(sp, tft, mv, acc, stage, part, y)
-        for i in RING:
-            for k in (1, 0):
-                if (j, i, k) == (0, 0, 0):
-                    continue
-                xc = here.xs[i] + here.cores[k]
-                remote(part.at[y, xc], came.at[me], psend, precv, (coil, here.rows[j] + xc)).start()
-    came[me] = part[here.ys[0], here.xs[0] + here.core]
-    dirgs = dirg.at[pl.ds(0, 63 * 32)]
+        if j != 0:
+            swap(k, y).start()
+        if k != 0:
+            before = RING[k - 1]
+            swap(k - 1, here.ys[before]).wait_recv()
+            for i in range(4):
+                both = part[here.ys[before], i, core].astype(F32) + half[k - 1, i].astype(F32)
+                pair[k - 1, i] = both.astype(BF16)
+            for i in RING:
+                to = here.rows[before] + here.xs[i] + core
+                remote(pair.at[k - 1, here.xs[i] // 2], came.at[before * 4 + i - 4], psend, precv, (coil, to)).start()
+    for i in RING:
+        for k in (1, 0):
+            if (i, k) == (0, 0):
+                continue
+            to = here.xs[i] + here.cores[k]
+            remote(part.at[here.ys[0], here.xs[i] // 2, here.cores[k]], came.at[12 + i * 2 + k], psend, precv,
+                   (coil, here.rows[0] + to)).start()
+    came[12] = part[here.ys[0], mine_x, core]
+    dirgs = dirg.at[pl.ds(0, 62 * 32)]
     remote(dirgs, dirgs, gsend, brecv.at[0], (coil, sibling)).wait_send()
-    others = came.at[pl.ds(0, 31)]
+
+    @pl.when(edge)
+    def _():
+        two = dirg.at[pl.ds(0, 64)]
+        remote(two, two, asend, brecv.at[0], (coil, sibling)).wait_send()
+
+    others = came.at[pl.ds(0, 19)]
     remote(others, others, psend, precv, (coil, sibling)).wait_recv()
     for p in range(2):
         for s in range(2):
             total = came[0, p, s].astype(F32)
-            for q in range(1, 32):
+            for q in range(1, 20):
                 total = total + came[q, p, s].astype(F32)
             zsend[s, p] = total.astype(BF16)
     for j in (4, 3, 5, 2, 6, 1, 7):
@@ -300,6 +335,7 @@
         remote(zsend.at[s], zcame.at[z], zsend_sem, zrecv_sem, device).start()
     zcame[z] = zsend[hi]
     remote(others, others, psend, precv, (coil, sibling)).wait_send()
+    remote(half, half, hsend, hrecv.at[0], (coil, sibling)).wait_send()
     seven = zcame.at[pl.ds(0, 7)]
     remote(seven, seven, zsend_sem, zrecv_sem, (coil, sibling)).wait_recv()
     applied = []
@@ -319,14 +355,21 @@
         mine = jnp.where(lane == k, sums[k], mine)
     row[...] = mine
     rows[spoke] = mine
-    for across in (1, 0):
+
+    def share(to, sem, where):
+        remote(row, rows.at[spoke], sem, srecv, (where, to)).start()
+
+    @pl.when(edge)
+    def _():
         for j, i in STEPS:
             for k in (1, 0):
-                if (across, j, i, k) == (0, 0, 0, 0):
-                    continue
-                to = here.rows[j] + here.xs[i] + here.cores[k] + across * here.flip
-                where = 3 - coil if across else coil
-                remote(row, rows.at[spoke], ssend, srecv, (where, to)).start()
+                for where in nearest:
+                    share(here.rows[j] + here.xs[i] + here.cores[k] + here.flip, esend, where)
+
+    for j, i in STEPS:
+        for k in (1, 0):
+            if (j, i, k) != (0, 0, 0):
+                share(here.rows[j] + here.xs[i] + here.cores[k], ssend, coil)
     for r in range(4):
         for p in range(2):
             for k in range(2):
@@ -345,7 +388,12 @@
         for p in range(2):
             alpha_ref[r, p] = alpha
             beta_ref[r, p] = beta
-    remote(most, most, ssend, srecv, (coil, sibling)).wait_send()
+    plane = rows.at[pl.ds(0, 31)]
+    remote(plane, plane, ssend, srecv, (coil, sibling)).wait_send()
+
+    @pl.when(edge)
+    def _():
+        remote(rows, rows, esend, srecv, (coil, sibling)).wait_send()
 
 
 def solve_call(tile_index, direction, residual, maps, wave, wavep, w):
@@ -356,44 +404,47 @@
     return pl.pallas_call(
         solve_kernel,
         out_shape=(block, block, block),
-        in_specs=[pl.BlockSpec(memory_space=pltpu.SMEM)] + [hbm] * 6,
+        in_specs=[hbm] * 7,
         out_specs=(vm, vm, vm),
         scratch_shapes=[
+            pltpu.SMEM((8,), jnp.int32),
             pltpu.VMEM((4, 2, 2, 256), F32),
             pltpu.VMEM((4, 2, 2, 256), F32),
             pltpu.VMEM((32, 128), F32),
-            pltpu.VMEM((2048, 128), F32),
+            pltpu.VMEM((64 * 40, 128), F32),
             pltpu.VMEM((4, 2, 128, 128), F32),
             pltpu.VMEM((128, 512), BF16),
             pltpu.VMEM((512, 128), BF16),
             pltpu.VMEM((16, 128, 256), F32),
             pltpu.VMEM((1024, 256), BF16),
             pltpu.VMEM((1024, 256), BF16),
-            pltpu.VMEM((2, 2, 1024, 128), F32),
+            pltpu.VMEM((2, 2, 64 * 24, 128), F32),
             pltpu.VMEM((1024, 256), BF16),
             pltpu.VMEM((1024, 256), BF16),
             pltpu.VMEM((16, 128, 256), BF16),
             pltpu.VMEM((2, 2, 64, 128), F32),
-            pltpu.VMEM((2, 128, 128), F32),
+            pltpu.VMEM((2, 192, 128), F32),
             pltpu.VMEM((8, 128, 2048), BF16),
             pltpu.VMEM((32, 32, 2, 1024), BF16),
             pltpu.VMEM((512, 512), BF16),
             pltpu.VMEM((512, 512), BF16),
-            pltpu.VMEM((4, 8, 2, 2, 8, 256), BF16),
-            pltpu.VMEM((32, 2, 2, 8, 256), BF16),
+            pltpu.VMEM((4, 4, 2, 2, 2, 8, 256), BF16),
+            pltpu.VMEM((3, 4, 2, 2, 8, 256), BF16),
+            pltpu.VMEM((3, 4, 2, 2, 8, 256), BF16),
+            pltpu.VMEM((20, 2, 2, 8, 256), BF16),
             pltpu.VMEM((2, 2, 8, 256), BF16),
             pltpu.VMEM((8, 2, 8, 256), BF16),
             pltpu.VMEM((2, 8, 256), F32),
             pltpu.VMEM((2, 8, 256), F32),
             pltpu.VMEM((1, 128), F32),
             pltpu.VMEM((64, 1, 128), F32),
-            dma((13,)), dma, dma((64,)), dma((2,)), dma, dma, dma, dma, dma, dma,
+            dma((14,)), dma, dma((64,)), dma((2,)), dma, dma, dma((3,)), dma, dma, dma, dma, dma, dma, dma,
         ],
         compiler_params=pltpu.CompilerParams(
-            collective_id=0, has_side_effects=True, vmem_limit_bytes=60 * 2**20
+            collective_id=0, has_side_effects=True, vmem_limit_bytes=32 * 2**20
         ),
         name="solve",
-    )(tile_index, direction, residual, maps, wave, wavep, w)
+    )(*(pltpu.with_memory_space_constraint(v, pltpu.HBM) for v in (tile_index, direction, residual, maps, wave, wavep, w)))
 
 
 def maps_view(maps):

time: 51.5 us -> 48.2 us (0.936)
  Pallas kernels: 49 us -> 46.7 us
  other arithmetic: 1.4 us -> 0.64 us
    pallas_call x1, Pallas kernels: 49 us -> 46.7 us  [solve_call(): pl.pallas_call(solve_kernel, out_shape=(block, block, block), in_specs=[h...]
    add x1, other arithmetic: 1.4 us -> 0.64 us  [shards(): new_direction = new_residual + beta * direction]
where the time goes in v2:
time: 48.2 us; the launch traced here: 48.1 us
  Pallas kernels  46.7 us (97%)
  between operations  0.69 us (1%)
  other arithmetic  0.64 us (1%)
    pallas_call x1, Pallas kernels, solve_call(): pl.pallas_call(solve_kernel, out_shape=(block, block, block), in_specs=[h...  46.7 us

profile of v2, /device:TPU:1, one launch (start us, length us, event | category | flops | bytes accessed | tf_op | source)
XLA Modules:
  0.0 48.1 jit_solution(15471844755220422029)
XLA Ops:
  0.6 0.0 copy-start
  0.6 0.0 copy-start.1
  0.7 0.0 copy-start.2
  0.7 46.7 %solve.1 = (f32[4,2,2,256]{3,2,1,0:T(2,128)S(1)}, f32[4,2,2,256]{3,2,1,0:T(2,128)S(1)}, f32[4,2,2,256]{3,2,1,0:T(2,128)S(1)}) custom-call(s32[8]{0:T(128)} %tile_hbm.1, f32[4,2,2,256]{3,2,1,0:T(2,128)} %d_hbm.1, f32[4,2,2,256]{3,2,1,0:T(2,128)} %r_hbm.1, bf16[32,8,32,2,128]{4,3,2,1,0:T(2,128)(2,1)} %bitcast.5, bf16[512,512]{1,0:T(8,128)(2,1)} %constant.4.clone.wave_hbm, ...), custom_call_target="tpu_custom_call" | custom-call | tf_op jit(solution)/shard_map/solve/pallas_call | solution.py:404
  47.4 0.0 copy-done
  47.4 0.0 copy-done.1
  47.4 0.0 copy-done.2
  47.4 0.6 %multiply_add_fusion = (f32[4,2,2,256]{3,2,1,0:T(2,128)}, f32[4,2,2,256]{3,2,1,0:T(2,128)}, f32[4,2,2,256]{3,2,1,0:T(2,128)}) fusion(f32[4,2,2,256]{3,2,1,0:T(2,128)S(1)} %get-tuple-element.8, f32[4,2,2,256]{3,2,1,0:T(2,128)S(1)} %copy-done, f32[4,2,2,256]{3,2,1,0:T(2,128)S(1)} %copy-done.1, f32[4,2,2,256]{3,2,1,0:T(2,128)S(1)} %get-tuple-element.6, ...), kind=kLoop, calls=%fused_computation | loop fusion | flops 24576 | bytes 147456 | tf_op jit(solution)/shard_map/add | solution.py:463
Async XLA Ops:
  0.6 46.8 %copy-start = (f32[4,2,2,256]{3,2,1,0:T(2,128)S(1)}, f32[4,2,2,256]{3,2,1,0:T(2,128)}, u32[]{:S(2)}) copy-start(f32[4,2,2,256]{3,2,1,0:T(2,128)} %d_hbm.1) | copy-start | bytes 49156
  0.6 46.8 %copy-start.1 = (f32[4,2,2,256]{3,2,1,0:T(2,128)S(1)}, f32[4,2,2,256]{3,2,1,0:T(2,128)}, u32[]{:S(2)}) copy-start(f32[4,2,2,256]{3,2,1,0:T(2,128)} %r_hbm.1) | copy-start | bytes 49156
  0.7 46.8 %copy-start.2 = (f32[4,2,2,256]{3,2,1,0:T(2,128)S(1)}, f32[4,2,2,256]{3,2,1,0:T(2,128)}, u32[]{:S(2)}) copy-start(f32[4,2,2,256]{3,2,1,0:T(2,128)} %param.8) | copy-start | bytes 49156

commit v3 on v2

--- a/solution.py
+++ b/solution.py
@@ -87,18 +87,29 @@
                     d[q, h, pl.ds(y * 32 + r, 8, stride=4), :] = dirg[pl.ds(base + h * 16 + r * 4 + q, 8, stride=40), :]
 
 
-def map_rows(mv, g, k):
-    v = mv[g, k].astype(F32)
-    return v[0:1].reshape(8, 128), v[1:2].reshape(8, 128)
-
-
-def forward_terms(mv, d, tf, side, i):
+def split_maps(mv, maps):
+    def split(k, carry):
+        for g in range(32):
+            v = mv[g, k].astype(F32)
+            maps[0, k, g * 8:(g + 1) * 8, :] = v[0:1].reshape(8, 128)
+            maps[1, k, g * 8:(g + 1) * 8, :] = v[1:2].reshape(8, 128)
+        return carry
+
+    lax.fori_loop(0, 32, split, 0)
+
+
+def map_rows(maps, k, start):
+    rows = pl.ds(pl.multiple_of(start, 8), 8)
+    return maps[0, k, rows, :], maps[1, k, rows, :]
+
+
+def forward_terms(maps, d, tf, side, i):
     p, c = i // 8, i % 8
     re, im = [], []
     for h in range(2):
         cr, ci = [], []
         for g in range(16):
-            mr, mi = map_rows(mv, (g // 4) * 8 + side * 4 + g % 4, c * 4 + p * 2 + h)
+            mr, mi = map_rows(maps, c * 4 + p * 2 + h, (g // 4) * 64 + side * 32 + g % 4 * 8)
             dr = d[2 * p, h, g * 8:(g + 1) * 8, :]
             di = d[2 * p + 1, h, g * 8:(g + 1) * 8, :]
             cr.append(mr * dr - mi * di)
@@ -139,7 +150,7 @@
         for r in range(8):
             rows = pl.ds(b * 8 + r, 16, stride=72)
             parts.append(jnp.concatenate([strided(ks, 0, rows), strided(ks, 1, rows)], 0).astype(BF16))
-        samples.append(dot(jnp.concatenate(parts, 1), wv[b], NT).astype(BF16))
+        samples.append(dot(wv[b], jnp.concatenate(parts, 1), NT).T.astype(BF16))
     for b in range(8):
         g = dot(samples[b], wv[b]).astype(BF16)
         for r in range(8):
@@ -154,40 +165,35 @@
         sp[i] = jnp.concatenate([strided(ks, 0, rows), strided(ks, 1, rows)], 0).astype(BF16)
 
 
-def combine_rows(sp, tft, mv, acc, stage, part, y):
+def combine_plane(sp, tft, maps, acc, stage, part, y, p):
     table = jnp.concatenate(
         [tft[pl.ds(pl.multiple_of(s * 256 + k * 128 + y * 32, 32), 32), :] for k in range(2) for s in range(2)], 0
     )
-
-    def plane(p, carry):
-        re = [[None] * 8, [None] * 8]
-        im = [[None] * 8, [None] * 8]
-        for c in range(8):
-            img = dot(table, sp[p * 8 + c])
-            for h in range(2):
-                for g in range(8):
-                    mr, mi = map_rows(mv, y * 8 + g, c * 4 + p * 2 + h)
-                    ir = img[g * 8:(g + 1) * 8, h * 128:(h + 1) * 128]
-                    ii = img[64 + g * 8:64 + (g + 1) * 8, h * 128:(h + 1) * 128]
-                    a, b = mr * ir + mi * ii, mr * ii - mi * ir
-                    re[h][g] = a if c == 0 else re[h][g] + a
-                    im[h][g] = b if c == 0 else im[h][g] + b
+    re = [[None] * 8, [None] * 8]
+    im = [[None] * 8, [None] * 8]
+    for c in range(8):
+        img = dot(table, sp[p * 8 + c])
         for h in range(2):
-            acc[0, h] = jnp.concatenate(re[h], 0)
-            acc[1, h] = jnp.concatenate(im[h], 0)
-            for s in range(2):
-                for k in range(2):
-                    for r in range(4):
-                        stage[h, pl.ds(s * 8 + k * 4 + r, 8, stride=24), :] = acc[k, h, pl.ds(s * 32 + r, 8, stride=4), :]
-            dense = jnp.concatenate([stage[h, i * 24:i * 24 + 16, :] for i in range(8)], 0)
-            part[y, :, :, p, :, :, h * 128:(h + 1) * 128] = dense.astype(BF16).reshape(4, 2, 2, 8, 128)
-        return carry
-
-    lax.fori_loop(0, 2, plane, 0)
+            for g in range(8):
+                mr, mi = map_rows(maps, c * 4 + p * 2 + h, y * 64 + g * 8)
+                ir = img[g * 8:(g + 1) * 8, h * 128:(h + 1) * 128]
+                ii = img[64 + g * 8:64 + (g + 1) * 8, h * 128:(h + 1) * 128]
+                a, b = mr * ir + mi * ii, mr * ii - mi * ir
+                re[h][g] = a if c == 0 else re[h][g] + a
+                im[h][g] = b if c == 0 else im[h][g] + b
+    for h in range(2):
+        acc[p, 0, h] = jnp.concatenate(re[h], 0)
+        acc[p, 1, h] = jnp.concatenate(im[h], 0)
+        for s in range(2):
+            for k in range(2):
+                for r in range(4):
+                    stage[p, h, pl.ds(s * 8 + k * 4 + r, 8, stride=24), :] = acc[p, k, h, pl.ds(s * 32 + r, 8, stride=4), :]
+        dense = jnp.concatenate([stage[p, h, i * 24:i * 24 + 16, :] for i in range(8)], 0)
+        part[y, :, :, p, :, :, h * 128:(h + 1) * 128] = dense.astype(BF16).reshape(4, 2, 2, 8, 128)
 
 
 def solve_kernel(tile_hbm, d_hbm, r_hbm, m_hbm, wave_hbm, wavep_hbm, w_hbm, applied_ref, alpha_ref, beta_ref,
-                 tile_ref, dv, rv, own, dirg, d, tf, tft, tacc, tr, ti, ks, gr, gi, sp, acc, stage, wv, mv, wave, wavep,
+                 tile_ref, dv, rv, own, dirg, d, tf, tft, tacc, tr, ti, ks, gr, gi, sp, acc, stage, wv, mv, maps, wave, wavep,
                  part, half, pair, came, zsend, zcame, d8, r8, row, rows,
                  load_sem, gsend, grecv, brecv, asend, hsend, hrecv, psend, precv, zsend_sem, zrecv_sem, ssend, srecv, esend):
     here = Place()
@@ -253,17 +259,18 @@
     send(slot(other), other, (coil, sibling), brecv.at[1])
     for step in STEPS[:15]:
         send(slot(other), other, (coil, here.chip(step)), grecv.at[other])
+    for load in loads[1:10]:
+        load.wait()
+    split_maps(mv, maps)
     for step in STEPS[:15]:
         s = here.chip(step)
         arrived(s)
         send(slot(s), s, (coil, sibling), brecv.at[0])
     relayed(0)
     unpack_direction(dirg, d, hi)
-    for load in loads[1:10]:
-        load.wait()
     for k in range(4):
         def first_half(i, carry):
-            tacc[i] = forward_terms(mv, d, tf, hi, i)
+            tacc[i] = forward_terms(maps, d, tf, hi, i)
             return carry
 
         lax.fori_loop(4 * k, 4 * k + 4, first_half, 0, unroll=4)
@@ -275,7 +282,7 @@
     unpack_direction(dirg, d, 1 - hi)
 
     def second_half(i, carry):
-        t = tacc[i] + forward_terms(mv, d, tf, 1 - hi, i)
+        t = tacc[i] + forward_terms(maps, d, tf, 1 - hi, i)
         where = pl.ds(pl.multiple_of(i * 64, 64), 64)
         tr[where, :] = t[:64].astype(BF16)
         ti[where, :] = t[64:].astype(BF16)
@@ -292,28 +299,26 @@
     def swap(k, y):
         return remote(part.at[y, :, 1 - core], half.at[k], hsend, hrecv.at[k], (coil, sibling))
 
+    def send_pair(k):
+        j = RING[k]
+        swap(k, here.ys[j]).wait_recv()
+        for i in range(4):
+            pair[k, i] = (part[here.ys[j], i, core].astype(F32) + half[k, i].astype(F32)).astype(BF16)
+        for i in RING:
+            if (j, i) != (0, 0):
+                to = here.rows[j] + here.xs[i] + core
+                remote(pair.at[k, here.xs[i] // 2], came.at[k * 4 + i], psend, precv, (coil, to)).start()
+
     for k, j in enumerate(RING):
         y = here.ys[j]
-        combine_rows(sp, tft, mv, acc, stage, part, y)
-        if j != 0:
-            swap(k, y).start()
-        if k != 0:
-            before = RING[k - 1]
-            swap(k - 1, here.ys[before]).wait_recv()
-            for i in range(4):
-                both = part[here.ys[before], i, core].astype(F32) + half[k - 1, i].astype(F32)
-                pair[k - 1, i] = both.astype(BF16)
-            for i in RING:
-                to = here.rows[before] + here.xs[i] + core
-                remote(pair.at[k - 1, here.xs[i] // 2], came.at[before * 4 + i - 4], psend, precv, (coil, to)).start()
-    for i in RING:
-        for k in (1, 0):
-            if (i, k) == (0, 0):
-                continue
-            to = here.xs[i] + here.cores[k]
-            remote(part.at[here.ys[0], here.xs[i] // 2, here.cores[k]], came.at[12 + i * 2 + k], psend, precv,
-                   (coil, here.rows[0] + to)).start()
-    came[12] = part[here.ys[0], mine_x, core]
+        combine_plane(sp, tft, maps, acc, stage, part, y, 0)
+        if k >= 2:
+            send_pair(k - 2)
+        combine_plane(sp, tft, maps, acc, stage, part, y, 1)
+        swap(k, y).start()
+    send_pair(2)
+    send_pair(3)
+    came[12] = pair[3, mine_x]
     dirgs = dirg.at[pl.ds(0, 62 * 32)]
     remote(dirgs, dirgs, gsend, brecv.at[0], (coil, sibling)).wait_send()
 
@@ -322,12 +327,12 @@
         two = dirg.at[pl.ds(0, 64)]
         remote(two, two, asend, brecv.at[0], (coil, sibling)).wait_send()
 
-    others = came.at[pl.ds(0, 19)]
+    others = came.at[pl.ds(0, 15)]
     remote(others, others, psend, precv, (coil, sibling)).wait_recv()
     for p in range(2):
         for s in range(2):
             total = came[0, p, s].astype(F32)
-            for q in range(1, 20):
+            for q in range(1, 16):
                 total = total + came[q, p, s].astype(F32)
             zsend[s, p] = total.astype(BF16)
     for j in (4, 3, 5, 2, 6, 1, 7):
@@ -422,26 +427,27 @@
             pltpu.VMEM((1024, 256), BF16),
             pltpu.VMEM((1024, 256), BF16),
             pltpu.VMEM((16, 128, 256), BF16),
-            pltpu.VMEM((2, 2, 64, 128), F32),
-            pltpu.VMEM((2, 192, 128), F32),
+            pltpu.VMEM((2, 2, 2, 64, 128), F32),
+            pltpu.VMEM((2, 2, 192, 128), F32),
             pltpu.VMEM((8, 128, 2048), BF16),
             pltpu.VMEM((32, 32, 2, 1024), BF16),
+            pltpu.VMEM((2, 32, 256, 128), F32),
             pltpu.VMEM((512, 512), BF16),
             pltpu.VMEM((512, 512), BF16),
             pltpu.VMEM((4, 4, 2, 2, 2, 8, 256), BF16),
-            pltpu.VMEM((3, 4, 2, 2, 8, 256), BF16),
-            pltpu.VMEM((3, 4, 2, 2, 8, 256), BF16),
-            pltpu.VMEM((20, 2, 2, 8, 256), BF16),
+            pltpu.VMEM((4, 4, 2, 2, 8, 256), BF16),
+            pltpu.VMEM((4, 4, 2, 2, 8, 256), BF16),
+            pltpu.VMEM((16, 2, 2, 8, 256), BF16),
             pltpu.VMEM((2, 2, 8, 256), BF16),
             pltpu.VMEM((8, 2, 8, 256), BF16),
             pltpu.VMEM((2, 8, 256), F32),
             pltpu.VMEM((2, 8, 256), F32),
             pltpu.VMEM((1, 128), F32),
             pltpu.VMEM((64, 1, 128), F32),
-            dma((14,)), dma, dma((64,)), dma((2,)), dma, dma, dma((3,)), dma, dma, dma, dma, dma, dma, dma,
+            dma((14,)), dma, dma((64,)), dma((2,)), dma, dma, dma((4,)), dma, dma, dma, dma, dma, dma, dma,
         ],
         compiler_params=pltpu.CompilerParams(
-            collective_id=0, has_side_effects=True, vmem_limit_bytes=32 * 2**20
+            collective_id=0, has_side_effects=True, vmem_limit_bytes=44 * 2**20
         ),
         name="solve",
     )(*(pltpu.with_memory_space_constraint(v, pltpu.HBM) for v in (tile_index, direction, residual, maps, wave, wavep, w)))

time: 48.2 us -> 46.3 us (0.961)
  Pallas kernels: 46.7 us -> 44.9 us
    pallas_call x1, Pallas kernels: 46.7 us -> 44.9 us  [solve_call(): pl.pallas_call(solve_kernel, out_shape=(block, block, block), in_specs=[h...]
where the time goes in v3:
time: 46.3 us; the launch traced here: 46.2 us
  Pallas kernels  44.9 us (97%)
  between operations  0.69 us (1%)
  other arithmetic  0.64 us (1%)
    pallas_call x1, Pallas kernels, solve_call(): pl.pallas_call(solve_kernel, out_shape=(block, block, block), in_specs=[h...  44.9 us

profile of v3, /device:TPU:1, one launch (start us, length us, event | category | flops | bytes accessed | tf_op | source)
XLA Modules:
  0.0 46.2 jit_solution(12655899820552239738)
XLA Ops:
  0.6 0.0 copy-start
  0.6 0.0 copy-start.1
  0.7 0.0 copy-start.2
  0.7 44.9 %solve.1 = (f32[4,2,2,256]{3,2,1,0:T(2,128)S(1)}, f32[4,2,2,256]{3,2,1,0:T(2,128)S(1)}, f32[4,2,2,256]{3,2,1,0:T(2,128)S(1)}) custom-call(s32[8]{0:T(128)} %tile_hbm.1, f32[4,2,2,256]{3,2,1,0:T(2,128)} %d_hbm.1, f32[4,2,2,256]{3,2,1,0:T(2,128)} %r_hbm.1, bf16[32,8,32,2,128]{4,3,2,1,0:T(2,128)(2,1)} %bitcast.5, bf16[512,512]{1,0:T(8,128)(2,1)} %constant.4.clone.wave_hbm, ...), custom_call_target="tpu_custom_call" | custom-call | tf_op jit(solution)/shard_map/solve/pallas_call | solution.py:409
  45.5 0.0 copy-done
  45.5 0.0 copy-done.1
  45.6 0.0 copy-done.2
  45.6 0.6 %multiply_add_fusion = (f32[4,2,2,256]{3,2,1,0:T(2,128)}, f32[4,2,2,256]{3,2,1,0:T(2,128)}, f32[4,2,2,256]{3,2,1,0:T(2,128)}) fusion(f32[4,2,2,256]{3,2,1,0:T(2,128)S(1)} %get-tuple-element.8, f32[4,2,2,256]{3,2,1,0:T(2,128)S(1)} %copy-done, f32[4,2,2,256]{3,2,1,0:T(2,128)S(1)} %copy-done.1, f32[4,2,2,256]{3,2,1,0:T(2,128)S(1)} %get-tuple-element.6, ...), kind=kLoop, calls=%fused_computation | loop fusion | flops 24576 | bytes 147456 | tf_op jit(solution)/shard_map/add | solution.py:469
Async XLA Ops:
  0.6 44.9 %copy-start = (f32[4,2,2,256]{3,2,1,0:T(2,128)S(1)}, f32[4,2,2,256]{3,2,1,0:T(2,128)}, u32[]{:S(2)}) copy-start(f32[4,2,2,256]{3,2,1,0:T(2,128)} %d_hbm.1) | copy-start | bytes 49156
  0.6 44.9 %copy-start.1 = (f32[4,2,2,256]{3,2,1,0:T(2,128)S(1)}, f32[4,2,2,256]{3,2,1,0:T(2,128)}, u32[]{:S(2)}) copy-start(f32[4,2,2,256]{3,2,1,0:T(2,128)} %r_hbm.1) | copy-start | bytes 49156
  0.7 44.9 %copy-start.2 = (f32[4,2,2,256]{3,2,1,0:T(2,128)S(1)}, f32[4,2,2,256]{3,2,1,0:T(2,128)}, u32[]{:S(2)}) copy-start(f32[4,2,2,256]{3,2,1,0:T(2,128)} %param.8) | copy-start | bytes 49156
